TPU v7x, 256 devices: a whole 4x4x8 slice. The times are simulated.
256 devices in a mesh: dp: 256 (over y, x, z, core).
Axes of the slice: x: 4, y: 4, z: 8, core: 2. Of those that a mesh axis runs over, the one named last changes fastest.
Arguments:
- image_emb: bfloat16 [2048, 1152], P('dp'), may hold values from -0.4375 to 0.4375
- text_tokens: bfloat16 [65536, 1152], P('dp'), may hold values from -0.078125 to 0.078125
- caption_ids: int32 [65536], P('dp'), may hold values from 0 to 2047, as said below
- groups: int32 [2048], P('dp'), may hold values from 0 to 511
- text_gain: float32 [1152], replicated, may hold values from 0.5 to 1.5
- log_scale: float32 [1], replicated, may hold values from 2 to 3
- logit_bias: float32 [1], replicated, may hold values from -3 to -1
Outputs:
- image_grad: float32 [2048, 1152], P('dp')
- token_grad: float32 [65536, 1152], P('dp')
- gain_grad: float32 [1152], replicated
- scalars: float32 [3], replicated
Inputs may be any that keep to these rules, and one draw needn't show every extreme that they name: `caption_ids`: caption ids never fall along the rows and every caption 0 .. 2047 has at least one row; the captions of the pairs of device d (ids 8 d to 8 (d + 1) - 1) all begin within the 256 rows of device d; the rows of device d before its first caption all belong to the last caption of device d - 1; device 0 begins with caption 0. `groups`: group ids of the pairs; equal ids mark matching pairs.
All inputs are finite; a program needn't handle non-finite values.
Results may differ from a plain program's by a relative error of at most 0.005.
Values may be sent and summed in bfloat16 or wider, within the bound.
No kernel may reach another device: no remote copies, remote signals or barrier semaphores. Data moves between devices by JAX's collectives and lax.ppermute only.
A program may use at most 64 MiB of HBM per device.

v0:
```python
import jax
import jax.numpy as jnp
from jax import lax
from jax.sharding import Mesh
from jax.sharding import PartitionSpec as P

DP = ("dp_0", "dp_1", "dp_2", "dp_3")


def from_behind(value, axis, by):
    count = lax.axis_size(axis)
    pairs = [(i, i + by) for i in range(count) if 0 <= i + by < count]
    return lax.ppermute(value, axis, pairs)


def side_by_side(arrays, axis, dim, along):
    ends, at = ([], 0)
    for a in arrays[:-1]:
        at += a.shape[along]
        ends.append(at)
    both = jnp.concatenate(arrays, axis=along)
    return tuple(jnp.split(lax.all_gather(both, axis, axis=dim, tiled=True), ends, axis=along))


def over_axes(value, axes):
    for axis in axes:
        value = lax.psum(value, axis)
    return value


def unit_rows(values):
    length = jnp.sqrt(jnp.sum(values * values, axis=1, keepdims=True))
    return (values / length, length)


def pair_margin(scaled, bias_value, row_groups, column_groups):
    labels = jnp.where(row_groups[:, None] == column_groups[None, :], 1.0, -1.0).astype(jnp.float32)
    margin = -labels * (scaled + bias_value)
    coeffs = -labels * jax.nn.sigmoid(margin)
    return (margin, coeffs)


def per_device(image_emb, text_tokens, caption_ids, groups, text_gain, log_scale, logit_bias):
    pairs_here = image_emb.shape[0]
    width_features = image_emb.shape[1]
    devices = lax.axis_size(DP)
    total_pairs = pairs_here * devices
    first_pair = lax.axis_index(DP) * pairs_here
    raw_image = image_emb.astype(jnp.float32)
    unit_image, image_norm = unit_rows(raw_image)
    image_low = unit_image.astype(jnp.bfloat16)
    local_ids = caption_ids - first_pair
    slot_index = lax.broadcasted_iota(jnp.int32, (1, pairs_here), 1)
    member = (local_ids[:, None] == slot_index).astype(jnp.bfloat16)
    pooled = lax.dot_general(
        member, text_tokens, (((0,), (0,)), ((), ())), preferred_element_type=jnp.float32
    )
    spilled = (local_ids == -1).astype(jnp.bfloat16)[None, :]
    spill_part = jnp.dot(spilled, text_tokens, preferred_element_type=jnp.float32)
    arrived = from_behind(spill_part, DP, -1)
    pooled = pooled.at[pairs_here - 1].add(arrived[0])
    embedded = pooled * text_gain[None, :]
    unit_text, text_norm = unit_rows(embedded)
    text_low = unit_text.astype(jnp.bfloat16)
    all_groups = lax.all_gather(groups, DP, axis=0, tiled=True)
    scale_value = jnp.exp(log_scale[0])
    bias_value = logit_bias[0]
    stored_width = 0
    initial = (
        jnp.zeros((pairs_here, width_features), jnp.float32),
        jnp.zeros((3,), jnp.float32),
        jnp.zeros((pairs_here, stored_width), jnp.bfloat16),
        jnp.zeros((pairs_here, width_features), jnp.float32),
    )
    block_rows, block_images = side_by_side((text_low, image_low), DP, 0, 1)
    scaled = scale_value * lax.dot_general(
        image_low, block_rows, (((1,), (1,)), ((), ())), preferred_element_type=jnp.float32
    )
    margin, coeffs = pair_margin(scaled, bias_value, groups, all_groups)
    coeff_low = coeffs.astype(jnp.bfloat16)
    image_acc = jnp.dot(coeff_low, block_rows, preferred_element_type=jnp.float32)
    sum_terms = jnp.stack(
        [jnp.sum(jax.nn.softplus(margin)), jnp.sum(coeffs * scaled), jnp.sum(coeffs)]
    )
    stored = initial[2]
    back_scaled = scale_value * lax.dot_general(
        block_images, text_low, (((1,), (1,)), ((), ())), preferred_element_type=jnp.float32
    )
    back_margin, back_coeffs = pair_margin(back_scaled, bias_value, all_groups, groups)
    back_low = back_coeffs.astype(jnp.bfloat16)
    carried = lax.dot_general(
        back_low, block_images, (((0,), (0,)), ((), ())), preferred_element_type=jnp.float32
    )
    image_acc, sum_terms, stored, carried = (image_acc, sum_terms, stored, carried)
    image_unit_grad = scale_value * image_acc
    text_unit_grad = scale_value * carried
    image_grad = (
        image_unit_grad - unit_image * jnp.sum(unit_image * image_unit_grad, axis=1, keepdims=True)
    ) / image_norm
    embed_grad = (
        text_unit_grad - unit_text * jnp.sum(unit_text * text_unit_grad, axis=1, keepdims=True)
    ) / text_norm
    gain_part = jnp.sum(embed_grad * pooled, axis=0)
    pooled_grad = embed_grad * text_gain[None, :]
    behind = from_behind(pooled_grad[pairs_here - 1 :], DP, 1)
    grad_table = jnp.concatenate([behind, pooled_grad], axis=0)
    token_grad = jnp.take(grad_table, local_ids + 1, axis=0)
    sum_terms, gain_grad = (over_axes(sum_terms, DP), over_axes(gain_part, DP))
    scalars = sum_terms / float(total_pairs * total_pairs)
    return (image_grad, token_grad, gain_grad, scalars)


def solution(mesh):
    finer = Mesh(mesh.devices.reshape(4, 4, 8, 2), ("dp_0", "dp_1", "dp_2", "dp_3"))
    placed = (P(DP, None), P(DP, None), P(DP), P(DP), P(), P(), P())
    return jax.shard_map(
        per_device,
        mesh=finer,
        in_specs=placed,
        out_specs=(P(DP, None), P(DP, None), P(), P()),
        check_vma=False,
    )
```

profile of v0, /device:TPU:1, one launch (start us, length us, event | category | flops | bytes accessed | tf_op | source)
XLA Modules:
  0.0 208.8 jit_solution(15179221970684075022)
XLA Ops:
  7.2 0.0 copy-start
  7.2 0.0 all-gather.2.cloned.1.call-start
  7.2 0.7 compare_and_fusion
  8.0 0.3 copy-done
  8.3 0.2 fusion.67
  8.4 5.1 %collective-permute-start = (f32[1,1152]{1,0:T(1,128)S(1)}, f32[1,1152]{1,0:T(1,128)S(1)}, u32[]{:S(2)}, u32[]{:S(2)}) collective-permute-start(f32[1,1152]{1,0:T(1,128)S(1)} %fusion.67), channel_id=1, source_target_pairs={{1,0},{2,1},{3,2},{4,3},{5,4},{6,5},{7,6},{8,7},{9,8},{10,9},{11,1... | collective-permute-start | bytes 13832 | tf_op jit(solution)/shard_map/ppermute | solution.py:13
  13.6 0.3 fusion.55
  13.9 0.9 fusion.58
  14.7 0.0 collective-permute-done
  14.7 0.1 scatter-add.4
  14.9 0.8 multiply_reduce_fusion.4
  15.7 0.8 fusion.62
  16.5 0.6 pad_maximum_fusion.1
  17.1 0.0 all-gather.2.cloned.1.call-update
  18.5 0.9 dynamic-update-slice.3
  19.4 83.6 %all-reduce = s32[2048]{0:T(1024)S(1)} all-reduce(s32[2048]{0:T(1024)S(1)} %dynamic-update-slice.3), channel_id=1, replica_groups=mesh['dp_0'=4,'dp_1'=4,'dp_2'=8,'dp_3'=2] {'dp_0','dp_1','dp_2','dp_3'}, use_global_device_ids=true, to_apply=%add | all-reduce | flops 2048 | bytes 16384
  103.0 37.6 %all-gather.2.cloned.1.call-done = bf16[2048,2304]{1,0:T(8,128)(2,1)} async-done(((bf16[8,2304]{1,0:T(8,128)(2,1)}), bf16[2048,2304]{1,0:T(8,128)(2,1)}) %all-gather.2.cloned.1.call-update) | async-done | bytes 9437200 | tf_op jit(solution)/shard_map/all_gather | solution.py:22
  140.6 6.7 %multiply_reduce_fusion.2 = (f32[8]{0:T(128)S(1)}, f32[8,1152]{1,0:T(8,128)S(1)}) fusion(f32[8]{0:T(128)S(1)} %sqrt.17, f32[8,1152]{1,0:T(8,128)S(1)} %scatter-add.4, f32[1152]{0:T(1024)} %param.13, bf16[2048,2304]{1,0:T(8,128)(2,1)} %all-gather.2.cloned.1.call-done, bf16[8,1152]{1,0:T(8,128)(2,1)S(1)} %get-tuple-element.37, f32[]{:T(128)} %bitcast.11, ...), kind=kOutput, calls=%fused_computation.47 | convolution fusion | flops 75723768 | bytes 9547840 | tf_op jit(solution)/shard_map/dot_general | solution.py:91
  147.3 0.1 multiply_reduce_fusion.1
  147.4 2.8 %collective-permute-start.1 = (f32[1,1152]{1,0:T(1,128)S(1)}, f32[1,1152]{1,0:T(1,128)S(1)}, u32[]{:S(2)}, u32[]{:S(2)}) collective-permute-start(f32[1,1152]{1,0:T(1,128)S(1)} %slice.25), channel_id=1, source_target_pairs={{0,1},{1,2},{2,3},{3,4},{4,5},{5,6},{6,7},{7,8},{8,9},{9,10},{10,1... | collective-permute-start | bytes 13832 | tf_op jit(solution)/shard_map/ppermute | solution.py:13
  150.3 4.4 %fusion.56 = (f32[]{:T(128)}, f32[]{:T(128)}, f32[]{:T(128)}, f32[8,2048]{1,0:T(8,128)S(1)}) fusion(f32[]{:T(128)} %bitcast.12, s32[2048]{0:T(1024)S(1)} %all-reduce, s32[8]{0:T(128)S(1)} %copy-done.3, bf16[8,1152]{1,0:T(8,128)(2,1)S(1)} %get-tuple-element.36, bf16[2048,2304]{1,0:T(8,128)(2,1)} %all-gather.2.cloned.1.call-done, f32[]{:T(128)} %bitcast), kind=kOutput, calls=%fused_computation.35 | convolution fusion | flops 38076416 | bytes 4811820 | tf_op jit(solution)/shard_map/dot_general | solution.py:76
  154.7 3.2 %multiply_reduce_fusion.3 = (f32[8]{0:T(128)S(1)}, f32[8,1152]{1,0:T(8,128)S(1)}) fusion(f32[8]{0:T(128)S(1)} %sqrt.16, bf16[8,1152]{1,0:T(8,128)(2,1)S(1)} %copy-done.1, bf16[2048,2304]{1,0:T(8,128)(2,1)} %all-gather.2.cloned.1.call-done, f32[8,2048]{1,0:T(8,128)S(1)} %get-tuple-element.35, f32[]{:T(128)} %bitcast.10, s32[2048]{0:T(1024)S(1)} %all-reduce, ...), kind=kOutput, calls=%fused_computation.49 | convolution fusion | flops 37958648 | bytes 4848736 | tf_op jit(solution)/shard_map/dot_general | solution.py:81
  157.9 0.7 subtract_divide_fusion.1
  158.6 2.0 pad_maximum_fusion.2
  160.6 9.1 %all-reduce.3 = (f32[1152]{0:T(1024)S(1)}, f32[3]{0:T(128)S(1)}) all-reduce(f32[1152]{0:T(1024)S(1)} %get-tuple-element.29, f32[3]{0:T(128)S(1)} %pad_maximum_fusion.2), channel_id=1, replica_groups=mesh['dp_0'=4,'dp_1'=4,'dp_2'=8,'dp_3'=2] {'dp_0'}, use_global_device_ids=true, to_apply=%region_5.6 | all-reduce | flops 1155 | bytes 9240 | tf_op jit(solution)/shard_map/psum | solution.py:27
  169.7 7.2 %all-reduce.2 = (f32[1152]{0:T(1024)S(1)}, f32[3]{0:T(128)S(1)}) all-reduce(f32[1152]{0:T(1024)S(1)} %get-tuple-element.23, f32[3]{0:T(128)S(1)} %get-tuple-element.24), channel_id=1, replica_groups=mesh['dp_0'=4,'dp_1'=4,'dp_2'=8,'dp_3'=2] {'dp_1'}, use_global_device_ids=true, to_apply=%region_6.7 | all-reduce | flops 1155 | bytes 9240 | tf_op jit(solution)/shard_map/psum | solution.py:27
  176.9 14.2 %all-reduce.1 = (f32[1152]{0:T(1024)S(1)}, f32[3]{0:T(128)S(1)}) all-reduce(f32[1152]{0:T(1024)S(1)} %get-tuple-element.21, f32[3]{0:T(128)S(1)} %get-tuple-element.22), channel_id=1, replica_groups=mesh['dp_0'=4,'dp_1'=4,'dp_2'=8,'dp_3'=2] {'dp_2'}, use_global_device_ids=true, to_apply=%region_7.8 | all-reduce | flops 1155 | bytes 9240 | tf_op jit(solution)/shard_map/psum | solution.py:27
  191.1 8.0 %all-reduce.4 = (f32[1152]{0:T(1024)}, f32[3]{0:T(128)S(1)}) all-reduce(f32[1152]{0:T(1024)S(1)} %get-tuple-element.19, f32[3]{0:T(128)S(1)} %get-tuple-element.20), channel_id=1, replica_groups=mesh['dp_0'=4,'dp_1'=4,'dp_2'=8,'dp_3'=2] {'dp_3'}, use_global_device_ids=true, to_apply=%region_8.9 | all-reduce | flops 1155 | bytes 9240 | tf_op jit(solution)/shard_map/psum | solution.py:27
  199.1 0.5 broadcast_multiply_fusion.1
  199.6 0.0 collective-permute-done.1
  199.6 1.2 gather_fusion
  200.8 1.2 broadcast_select_fusion
  (16 shorter events, 0.1 us)
Async XLA Ops:
  7.2 1.1 copy-start
  7.2 133.4 %all-gather.2.cloned.1.call-start = ((), (), s32[]{:S(2)}) async-start(), calls=%async_computation | async-start | bytes 9474048 | tf_op jit(solution)/shard_map/all_gather | solution.py:22
  8.4 6.3 %collective-permute-start = (f32[1,1152]{1,0:T(1,128)S(1)}, f32[1,1152]{1,0:T(1,128)S(1)}, u32[]{:S(2)}, u32[]{:S(2)}) collective-permute-start(f32[1,1152]{1,0:T(1,128)S(1)} %fusion.67), channel_id=1, source_target_pairs={{1,0},{2,1},{3,2},{4,3},{5,4},{6,5},{7,6},{8,7},{9,8},{10,9},{11,1... | collective-permute-start | bytes 13832 | tf_op jit(solution)/shard_map/ppermute | solution.py:13
  140.6 6.7 %copy-start.2 = (f32[1152]{0:T(1024)S(1)}, f32[1152]{0:T(1024)}, u32[]{:S(2)}) copy-start(f32[1152]{0:T(1024)} %param.13) | copy-start | bytes 13828
  140.6 9.7 %copy-start.3 = (s32[8]{0:T(128)S(1)}, s32[8]{0:T(128)}, u32[]{:S(2)}) copy-start(s32[8]{0:T(128)} %param.12) | copy-start | bytes 100
  147.3 7.3 %copy-start.1 = (bf16[8,1152]{1,0:T(8,128)(2,1)S(1)}, bf16[8,1152]{1,0:T(8,128)(2,1)}, u32[]{:S(2)}) copy-start(bf16[8,1152]{1,0:T(8,128)(2,1)} %param.9) | copy-start | bytes 55300
  147.4 52.2 %collective-permute-start.1 = (f32[1,1152]{1,0:T(1,128)S(1)}, f32[1,1152]{1,0:T(1,128)S(1)}, u32[]{:S(2)}, u32[]{:S(2)}) collective-permute-start(f32[1,1152]{1,0:T(1,128)S(1)} %slice.25), channel_id=1, source_target_pairs={{0,1},{1,2},{2,3},{3,4},{4,5},{5,6},{6,7},{7,8},{8,9},{9,10},{10,1... | collective-permute-start | bytes 13832 | tf_op jit(solution)/shard_map/ppermute | solution.py:13
Sparse Core Ops, SparseCore 0:
  17.3 123.2 all-gather.1
where the time goes:
time: 209 us
  blocking collectives  122 us (58%)
  waiting for transfers between devices  37.6 us (18%)
  between operations  15.5 us (7%)
  matrix products  14.8 us (7%)
  other arithmetic  8.39 us (4%)
  starting transfers between devices  7.96 us (4%)
  local copies, waits for them, and re-layouts  2.51 us (1%)
    unnamed x1, blocking collectives  83.6 us
    psum x4, blocking collectives, over_axes(): value = lax.psum(value, axis)  38.5 us
    all_gather x1, waiting for transfers between devices, side_by_side(): lax.all_gather(both, axis, axis=dim, tiled=True)  37.6 us
    ppermute x2, starting transfers between devices, from_behind(): return lax.ppermute(value, axis, pairs)  7.93 us
    dot_general x1, matrix products, per_device(): lax.dot_general(back_low, block_images, (((0,), (0,)), ((), ())), preferr...  6.7 us
    dot_general x1, matrix products, per_device(): lax.dot_general(image_low, block_rows, (((1,), (1,)), ((), ())), preferre...  4.38 us
  transfers between devices with their start and end apart: 3, of which 1 were waited for; matrix products, arithmetic and copies ran while one was open for 6% of the time, Pallas kernels for 0%

commit v1 on v0

--- a/solution.py
+++ b/solution.py
@@ -5,6 +5,10 @@
 from jax.sharding import PartitionSpec as P
 
 DP = ("dp_0", "dp_1", "dp_2", "dp_3")
+
+
+def close_grid(chunk, peer_axis):
+    return jax.lax.all_gather(chunk, axis_name=peer_axis).sum(axis=0)
 
 
 def from_behind(value, axis, by):
@@ -24,7 +28,7 @@
 
 def over_axes(value, axes):
     for axis in axes:
-        value = lax.psum(value, axis)
+        value = close_grid(value, peer_axis=axis)
     return value
 
 

time: 209 us -> 260 us (1.24)
  blocking collectives: 122 us -> 171 us
  waiting for transfers between devices: 37.6 us -> 30.1 us
  local copies, waits for them, and re-layouts: 2.51 us -> 8.71 us
  between operations: 15.5 us -> 18.1 us
    all_gather x0 -> x4, blocking collectives: none -> 45.3 us  [close_grid(): return jax.lax.all_gather(chunk, axis_name=peer_axis).sum(axis=0)]
    unnamed x1 -> x5, blocking collectives: 83.6 us -> 125 us
    psum x4 -> x0, blocking collectives: 38.5 us -> none  [over_axes(): value = lax.psum(value, axis)]
    all_gather x1, waiting for transfers between devices: 37.6 us -> 30.1 us  [side_by_side(): lax.all_gather(both, axis, axis=dim, tiled=True)]
    unnamed x10 -> x25, local copies, waits for them, and re-layouts: 1.15 us -> 7.01 us
  transfers between devices with their start and end apart: 3 -> 3, of which waited for: 1 -> 1; matrix products, arithmetic and copies ran while one was open for 6% -> 8% of each run, Pallas kernels for 0% -> 0%
where the time goes in v1:
time: 260 us; the launch traced here: 259 us
  blocking collectives  171 us (66%)
  waiting for transfers between devices  30.1 us (12%)
  between operations  18.1 us (7%)
  matrix products  14.1 us (5%)
  other arithmetic  9.3 us (4%)
  local copies, waits for them, and re-layouts  8.71 us (3%)
  starting transfers between devices  7.97 us (3%)
    unnamed x5, blocking collectives  125 us
    all_gather x4, blocking collectives, close_grid(): return jax.lax.all_gather(chunk, axis_name=peer_axis).sum(axis=0)  45.3 us
    all_gather x1, waiting for transfers between devices, side_by_side(): lax.all_gather(both, axis, axis=dim, tiled=True)  30.1 us
    ppermute x2, starting transfers between devices, from_behind(): return lax.ppermute(value, axis, pairs)  7.93 us
    unnamed x25, local copies, waits for them, and re-layouts  7.01 us
    dot_general x1, matrix products, per_device(): lax.dot_general(back_low, block_images, (((0,), (0,)), ((), ())), preferr...  6.04 us
  transfers between devices with their start and end apart: 3, of which 1 were waited for; matrix products, arithmetic and copies ran while one was open for 8% of the time, Pallas kernels for 0%

profile of v1, /device:TPU:1, one launch (start us, length us, event | category | flops | bytes accessed | tf_op | source)
XLA Modules:
  0.0 259.0 jit_solution(1743893375943543079)
XLA Ops:
  7.2 0.7 compare_and_fusion
  8.4 5.1 %collective-permute-start = (f32[1,1152]{1,0:T(1,128)S(1)}, f32[1,1152]{1,0:T(1,128)S(1)}, u32[]{:S(2)}, u32[]{:S(2)}) collective-permute-start(f32[1,1152]{1,0:T(1,128)S(1)} %fusion.67), channel_id=1, source_target_pairs={{1,0},{2,1},{3,2},{4,3},{5,4},{6,5},{7,6},{8,7},{9,8},{10,9},{11,1... | collective-permute-start | bytes 13832 | tf_op jit(solution)/shard_map/ppermute | solution.py:17
  13.6 0.3 fusion.46
  13.9 0.9 fusion.52
  14.9 0.8 multiply_reduce_fusion.4
  15.7 0.8 fusion.62
  16.5 0.6 pad_maximum_fusion.1
  18.5 1.3 dynamic-slice.7
  19.8 1.3 dynamic-slice.8
  22.4 1.3 dynamic-slice.9
  24.3 1.3 dynamic-slice.10
  26.2 0.9 dynamic-update-slice.3
  27.1 83.3 %all-reduce = s32[2048]{0:T(1024)S(1)} all-reduce(s32[2048]{0:T(1024)S(1)} %dynamic-update-slice.3), channel_id=1, replica_groups=mesh['dp_0'=4,'dp_1'=4,'dp_2'=8,'dp_3'=2] {'dp_0','dp_1','dp_2','dp_3'}, use_global_device_ids=true, to_apply=%add | all-reduce | flops 2048 | bytes 16384
  110.4 30.1 %all-gather.14.cloned.1.call-done = bf16[2048,2304]{1,0:T(8,128)(2,1)} async-done(((bf16[8,2304]{1,0:T(8,128)(2,1)}), bf16[2048,2304]{1,0:T(8,128)(2,1)}) %all-gather.14.cloned.1.call-update) | async-done | bytes 9437200 | tf_op jit(solution)/shard_map/all_gather | solution.py:26
  140.5 6.0 %multiply_reduce_fusion.2 = (f32[8]{0:T(128)S(1)}, f32[8,1152]{1,0:T(8,128)S(1)}) fusion(f32[8]{0:T(128)S(1)} %sqrt.17, f32[8,1152]{1,0:T(8,128)S(1)} %scatter-add.4, f32[1152]{0:T(1024)} %param.13, bf16[2048,2304]{1,0:T(8,128)(2,1)} %all-gather.14.cloned.1.call-done, bf16[8,1152]{1,0:T(8,128)(2,1)S(1)} %get-tuple-element.29, f32[]{:T(128)} %bitcast.15, ...), kind=kOutput, calls=%fused_computation.41 | convolution fusion | flops 75723768 | bytes 9547840 | tf_op jit(solution)/shard_map/dot_general | solution.py:95
  146.7 2.8 %collective-permute-start.1 = (f32[1,1152]{1,0:T(1,128)S(1)}, f32[1,1152]{1,0:T(1,128)S(1)}, u32[]{:S(2)}, u32[]{:S(2)}) collective-permute-start(f32[1,1152]{1,0:T(1,128)S(1)} %slice.25), channel_id=1, source_target_pairs={{0,1},{1,2},{2,3},{3,4},{4,5},{5,6},{6,7},{7,8},{8,9},{9,10},{10,1... | collective-permute-start | bytes 13832 | tf_op jit(solution)/shard_map/ppermute | solution.py:17
  149.6 9.7 %all-gather.8 = f32[4,1,1152]{2,1,0:T(1,128)S(1)} all-gather(f32[1,1,1152]{2,1,0:T(1,128)S(1)} %reshape.89), channel_id=2, replica_groups=mesh['dp_0'=4,'dp_1'=4,'dp_2'=8,'dp_3'=2] {'dp_0'}, dimensions={0}, use_global_device_ids=true | all-gather | bytes 23040 | tf_op jit(solution)/shard_map/all_gather | solution.py:11
  159.2 4.4 %fusion.47 = (f32[]{:T(128)}, f32[]{:T(128)}, f32[]{:T(128)}, f32[8,2048]{1,0:T(8,128)S(1)}) fusion(f32[]{:T(128)} %bitcast.16, s32[2048]{0:T(1024)S(1)} %all-reduce, s32[8]{0:T(128)S(1)} %copy-done.3, bf16[8,1152]{1,0:T(8,128)(2,1)S(1)} %get-tuple-element.28, bf16[2048,2304]{1,0:T(8,128)(2,1)} %all-gather.14.cloned.1.call-done, f32[]{:T(128)} %bitcast), kind=kOutput, calls=%fused_computation.26 | convolution fusion | flops 38076416 | bytes 4811820 | tf_op jit(solution)/shard_map/dot_general | solution.py:80
  163.6 2.1 maximum_dynamic-update-slice_fusion
  165.8 8.0 %all-reduce.1 = f32[12]{0:T(128)S(1)} all-reduce(f32[12]{0:T(128)S(1)} %maximum_dynamic-update-slice_fusion), channel_id=6, replica_groups=mesh['dp_0'=4,'dp_1'=4,'dp_2'=8,'dp_3'=2] {'dp_0'}, use_global_device_ids=true, to_apply=%add.1 | all-reduce | flops 12 | bytes 96
  174.2 9.1 %all-gather.9 = f32[4,1,1152]{2,1,0:T(1,128)S(1)} all-gather(f32[1,1,1152]{2,1,0:T(1,128)S(1)} %reshape.91), channel_id=3, replica_groups=mesh['dp_0'=4,'dp_1'=4,'dp_2'=8,'dp_3'=2] {'dp_1'}, dimensions={0}, use_global_device_ids=true | all-gather | bytes 23040 | tf_op jit(solution)/shard_map/all_gather | solution.py:11
  183.3 6.8 %all-reduce.2 = f32[12]{0:T(128)S(1)} all-reduce(f32[12]{0:T(128)S(1)} %dynamic-update-slice.5), channel_id=7, replica_groups=mesh['dp_0'=4,'dp_1'=4,'dp_2'=8,'dp_3'=2] {'dp_1'}, use_global_device_ids=true, to_apply=%add.2 | all-reduce | flops 12 | bytes 96
  190.4 13.9 %all-reduce.3 = f32[24]{0:T(128)S(1)} all-reduce(f32[24]{0:T(128)S(1)} %dynamic-update-slice.6), channel_id=8, replica_groups=mesh['dp_0'=4,'dp_1'=4,'dp_2'=8,'dp_3'=2] {'dp_2'}, use_global_device_ids=true, to_apply=%add.3 | all-reduce | flops 24 | bytes 192
  204.7 13.3 %all-reduce.4 = f32[6]{0:T(128)S(1)} all-reduce(f32[6]{0:T(128)S(1)} %dynamic-update-slice.7), channel_id=9, replica_groups=mesh['dp_0'=4,'dp_1'=4,'dp_2'=8,'dp_3'=2] {'dp_3'}, use_global_device_ids=true, to_apply=%add.4 | all-reduce | flops 6 | bytes 48
  218.1 0.5 broadcast_multiply_fusion.1
  218.6 3.2 %multiply_reduce_fusion.3 = (f32[8]{0:T(128)S(1)}, f32[8,1152]{1,0:T(8,128)S(1)}) fusion(f32[8]{0:T(128)S(1)} %sqrt.16, bf16[8,1152]{1,0:T(8,128)(2,1)S(1)} %copy-done.1, bf16[2048,2304]{1,0:T(8,128)(2,1)} %all-gather.14.cloned.1.call-done, f32[8,2048]{1,0:T(8,128)S(1)} %get-tuple-element.27, f32[]{:T(128)} %bitcast.14, s32[2048]{0:T(1024)S(1)} %all-reduce, ...), kind=kOutput, calls=%fused_computation.43 | convolution fusion | flops 37958648 | bytes 4848736 | tf_op jit(solution)/shard_map/dot_general | solution.py:85
  221.9 0.7 subtract_divide_fusion.1
  222.6 18.5 %all-gather.10 = f32[8,1,1152]{2,1,0:T(1,128)S(1)} all-gather(f32[1,1,1152]{2,1,0:T(1,128)S(1)} %reshape.93), channel_id=4, replica_groups=mesh['dp_0'=4,'dp_1'=4,'dp_2'=8,'dp_3'=2] {'dp_2'}, dimensions={0}, use_global_device_ids=true | all-gather | bytes 41472 | tf_op jit(solution)/shard_map/all_gather | solution.py:11
  241.2 8.0 %all-gather.11 = f32[2,1,1152]{2,1,0:T(1,128)S(1)} all-gather(f32[1,1,1152]{2,1,0:T(1,128)S(1)} %reshape.95), channel_id=5, replica_groups=mesh['dp_0'=4,'dp_1'=4,'dp_2'=8,'dp_3'=2] {'dp_3'}, dimensions={0}, use_global_device_ids=true | all-gather | bytes 13824 | tf_op jit(solution)/shard_map/all_gather | solution.py:11
  249.2 0.6 reduce_sum.152
  249.8 1.2 gather_fusion
  251.0 1.2 broadcast_select_fusion
  (47 shorter events, 2.1 us)
Async XLA Ops:
  7.2 1.1 copy-start
  7.2 133.4 %all-gather.14.cloned.1.call-start = ((), (), s32[]{:S(2)}) async-start(), calls=%async_computation | async-start | bytes 9474048 | tf_op jit(solution)/shard_map/all_gather | solution.py:26
  8.4 6.3 %collective-permute-start = (f32[1,1152]{1,0:T(1,128)S(1)}, f32[1,1152]{1,0:T(1,128)S(1)}, u32[]{:S(2)}, u32[]{:S(2)}) collective-permute-start(f32[1,1152]{1,0:T(1,128)S(1)} %fusion.67), channel_id=1, source_target_pairs={{1,0},{2,1},{3,2},{4,3},{5,4},{6,5},{7,6},{8,7},{9,8},{10,9},{11,1... | collective-permute-start | bytes 13832 | tf_op jit(solution)/shard_map/ppermute | solution.py:17
  140.5 6.1 %copy-start.2 = (f32[1152]{0:T(1024)S(1)}, f32[1152]{0:T(1024)}, u32[]{:S(2)}) copy-start(f32[1152]{0:T(1024)} %param.13) | copy-start | bytes 13828
  140.5 18.7 %copy-start.3 = (s32[8]{0:T(128)S(1)}, s32[8]{0:T(128)}, u32[]{:S(2)}) copy-start(s32[8]{0:T(128)} %param.12) | copy-start | bytes 100
  146.6 72.1 %copy-start.1 = (bf16[8,1152]{1,0:T(8,128)(2,1)S(1)}, bf16[8,1152]{1,0:T(8,128)(2,1)}, u32[]{:S(2)}) copy-start(bf16[8,1152]{1,0:T(8,128)(2,1)} %param.9) | copy-start | bytes 55300
  146.7 103.1 %collective-permute-start.1 = (f32[1,1152]{1,0:T(1,128)S(1)}, f32[1,1152]{1,0:T(1,128)S(1)}, u32[]{:S(2)}, u32[]{:S(2)}) collective-permute-start(f32[1,1152]{1,0:T(1,128)S(1)} %slice.25), channel_id=1, source_target_pairs={{0,1},{1,2},{2,3},{3,4},{4,5},{5,6},{6,7},{7,8},{8,9},{9,10},{10,1... | collective-permute-start | bytes 13832 | tf_op jit(solution)/shard_map/ppermute | solution.py:17
Sparse Core Ops, SparseCore 0:
  17.3 123.2 all-gather.13
